TPU v7x, 128 devices: a whole 4x4x4 slice. The times are simulated.
128 devices in a mesh: py: 4 (over z_hi, core), px: 8 (over z_lo, x), pz: 4 (over y).
Axes of the slice: x: 4, y: 4, z: 4 (z_hi: 2, z_lo: 2; z = z_hi * 2 + z_lo), core: 2. Of those that a mesh axis runs over, the one named last changes fastest.
Arguments:
- density: float32 [32, 512, 128, 128], P('py', 'px', 'pz'), may hold values from 0.2 to 1.8
- crowding: float32 [32, 512, 128, 128], P('py', 'px', 'pz'), may hold values from 0.5 to 2
Outputs:
- column_sum: float32 [32, 512, 128, 128], P('py', 'px', 'pz')
- density_end: float32 [32, 512, 128, 128], P('py', 'px', 'pz')
All inputs are finite; a program needn't handle non-finite values.
Results may differ from a plain program's by a relative error of at most 0.00002.
Values sent between devices are 32-bit elements; how exact they have to be, the bound alone decides.
A program may use at most 320 MiB of HBM per device.

v0:
```python
import jax
import jax.numpy as jnp
from jax import lax
from jax.sharding import PartitionSpec as P

STEPS = 6


def with_halo(array, sides, width):
    edges = {}
    for axis, dim in sides:
        size, length = (lax.axis_size(axis), array.shape[dim])
        up = [(i, (i + 1) % size) for i in range(size - 1)]
        last = lax.slice_in_dim(array, length - width, length, axis=dim)
        leading = lax.slice_in_dim(array, 0, width, axis=dim)
        edges[dim] = (
            lax.ppermute(last, axis, up),
            lax.ppermute(leading, axis, [(b, a) for a, b in up]),
        )
    done = []
    for _, dim in sides:
        low, high = edges[dim]
        around = [(width, width) if d in done else (0, 0) for d in range(array.ndim)]
        array = jnp.concatenate([jnp.pad(low, around), array, jnp.pad(high, around)], axis=dim)
        done.append(dim)
    return array


def entering(part, axis, combine, identity):
    place = lax.axis_index(axis)
    gathered = lax.all_gather(part, axis)
    state = jnp.zeros_like(part) + jnp.asarray(identity, part.dtype)

    def one(turn, state):
        return combine(state, lax.dynamic_index_in_dim(gathered, turn, 0, False))

    return lax.fori_loop(0, place, one, state)


def without_rim(values, dims):
    for dim in dims:
        values = lax.slice_in_dim(values, 1, values.shape[dim] - 1, axis=dim)
    return values


def shifted_cells(values, dim, start, dims):
    others = [other for other in dims if other != dim]
    values = without_rim(values, others)
    return lax.slice_in_dim(values, start, start + values.shape[dim] - 2, axis=dim)


def march_step(padded, crowding):
    middle = without_rim(padded, (0, 1, 2))
    lower = [shifted_cells(padded, dim, 0, (0, 1, 2)) for dim in (0, 1, 2)]
    upper = [shifted_cells(padded, dim, 2, (0, 1, 2)) for dim in (0, 1, 2)]
    spread = lower[0] + upper[0] + lower[1] + upper[1] + lower[2] + upper[2] - 6.0 * middle
    return middle + 0.1 * spread + 0.2 * middle * (1.0 - middle * crowding)


def local(density, crowding):
    for step in range(STEPS):
        padded = with_halo(density, (("py", 0), ("px", 1), ("pz", 2)), 1)
        density = march_step(padded, crowding)
    here = jnp.cumsum(density, axis=0)
    total = lax.slice_in_dim(here, here.shape[0] - 1, here.shape[0], axis=0)

    def add_pair(earlier_total, later_total):
        return earlier_total + later_total

    below = entering(total, "py", add_pair, jnp.zeros_like(total))
    column_sum = (here + below) / (density.shape[0] * lax.axis_size("py"))
    return (column_sum, density)


def solution(mesh):
    return jax.shard_map(
        local,
        mesh=mesh,
        in_specs=(P("py", "px", "pz", None), P("py", "px", "pz", None)),
        out_specs=(P("py", "px", "pz", None), P("py", "px", "pz", None)),
        check_vma=False,
    )
```

profile of v0, /device:TPU:65, one launch (start us, length us, event | category | flops | bytes accessed | tf_op | source)
XLA Modules:
  0.0 398.8 jit_solution(4359192296500702847)
XLA Ops:
  7.2 1.9 fusion.83
  9.1 1.6 collective-permute-start
  10.7 3.3 collective-permute-start.1
  14.9 3.1 collective-permute-start.2
  19.4 2.6 fusion.81
  22.0 3.2 collective-permute-start.4
  27.7 4.6 %constant_dynamic-update-slice_fusion.1 = f32[10,64,32,128]{3,2,1,0:T(8,128)} fusion(f32[10,64,32,128]{3,2,1,0:T(8,128)} %constant_dynamic-update-slice_fusion.2, f32[8,64,32,128]{3,2,1,0:T(8,128)S(1)} %copy-done), kind=kLoop, calls=%fused_computation.171 | loop fusion | bytes 16777216
  33.4 23.6 %fusion.60 = f32[8,64,32,128]{3,2,1,0:T(8,128)} fusion(f32[8,64,32,128]{3,2,1,0:T(8,128)} %param.4, f32[8,64,1,128]{3,2,1,0:T(1,128)S(1)} %bitcast.48, f32[10,1,32,128]{3,2,1,0:T(8,128)S(1)} %pad.75, f32[10,64,32,128]{3,2,1,0:T(8,128)} %constant_dynamic-update-slice_fusion, f32[10,1,32,128]{3,2,1,0:T(8,128)S(1)} %pad.74, f32[8,64,1,128]{3,2,1,0:T(1,128)S(1)} %bitcast.42, ...), kind=kLoop, calls=%fused_computation.152 | loop fusion | flops 62914560 | bytes 38600704 | tf_op jit(solution)/shard_map/add | solution.py:57
  57.0 1.7 fusion.79
  60.0 6.4 %collective-permute-start.7 = (f32[1,64,32,128]{3,2,1,0:T(8,128)S(1)}, f32[1,64,32,128]{3,2,1,0:T(8,128)S(1)}, u32[]{:S(2)}, u32[]{:S(2)}) collective-permute-start(f32[1,64,32,128]{3,2,1,0:T(8,128)S(1)} %get-tuple-element.75), channel_id=1, source_target_pairs={{32,0},{64,32},{96,64},{33,1},{65,33},{97,65},{34,2},{66,34},{98,6... | collective-permute-start | bytes 3145736 | tf_op jit(solution)/shard_map/ppermute | solution.py:18
  67.5 4.3 %collective-permute-start.8 = (f32[8,1,32,128]{3,2,1,0:T(8,128)S(1)}, f32[8,1,32,128]{3,2,1,0:T(8,128)S(1)}, u32[]{:S(2)}, u32[]{:S(2)}) collective-permute-start(f32[8,1,32,128]{3,2,1,0:T(8,128)S(1)} %get-tuple-element.76), channel_id=1, source_target_pairs={{0,4},{4,8},{8,12},{12,16},{16,20},{20,24},{24,28},{1,5},{5,9},{9,... | collective-permute-start | bytes 393224 | tf_op jit(solution)/shard_map/ppermute | solution.py:17
  71.7 2.6 fusion.78
  74.4 4.2 %collective-permute-start.10 = (f32[8,64,1,128]{3,1,2,0:T(8,128)S(1)}, f32[8,64,1,128]{3,1,2,0:T(8,128)S(1)}, u32[]{:S(2)}, u32[]{:S(2)}) collective-permute-start(f32[8,64,1,128]{3,1,2,0:T(8,128)S(1)} %bitcast.56), channel_id=1, source_target_pairs={{0,1},{1,2},{2,3},{4,5},{5,6},{6,7},{8,9},{9,10},{10,11},{12,13},{... | collective-permute-start | bytes 786440 | tf_op jit(solution)/shard_map/ppermute | solution.py:17
  81.2 4.4 %collective-permute-done.9 = f32[8,1,32,128]{3,2,1,0:T(8,128)S(1)} collective-permute-done((f32[8,1,32,128]{3,2,1,0:T(8,128)S(1)}, f32[8,1,32,128]{3,2,1,0:T(8,128)S(1)}, u32[]{:S(2)}, u32[]{:S(2)}) %collective-permute-start.9) | collective-permute-done | bytes 131104 | tf_op jit(solution)/shard_map/ppermute | solution.py:18
  85.7 23.7 %fusion.49 = f32[8,64,32,128]{3,2,1,0:T(8,128)} fusion(f32[8,64,32,128]{3,2,1,0:T(8,128)} %fusion.60, f32[8,64,1,128]{3,2,1,0:T(1,128)S(1)} %bitcast.43, f32[10,1,32,128]{3,2,1,0:T(8,128)S(1)} %pad.79, f32[10,1,32,128]{3,2,1,0:T(8,128)S(1)} %pad.78, f32[1,64,32,128]{3,2,1,0:T(8,128)S(1)} %collective-permute-done.7, ...), kind=kLoop, calls=%fused_computation.123 | loop fusion | flops 79691776 | bytes 28114944 | tf_op jit(solution)/shard_map/add | solution.py:57
  109.4 1.7 fusion.76
  112.4 7.5 %collective-permute-start.13 = (f32[1,64,32,128]{3,2,1,0:T(8,128)S(1)}, f32[1,64,32,128]{3,2,1,0:T(8,128)S(1)}, u32[]{:S(2)}, u32[]{:S(2)}) collective-permute-start(f32[1,64,32,128]{3,2,1,0:T(8,128)S(1)} %get-tuple-element.69), channel_id=1, source_target_pairs={{32,0},{64,32},{96,64},{33,1},{65,33},{97,65},{34,2},{66,34},{98,6... | collective-permute-start | bytes 3145736 | tf_op jit(solution)/shard_map/ppermute | solution.py:18
  120.9 3.1 collective-permute-start.14
  124.0 2.6 fusion.75
  126.7 4.3 %collective-permute-start.16 = (f32[8,64,1,128]{3,1,2,0:T(8,128)S(1)}, f32[8,64,1,128]{3,1,2,0:T(8,128)S(1)}, u32[]{:S(2)}, u32[]{:S(2)}) collective-permute-start(f32[8,64,1,128]{3,1,2,0:T(8,128)S(1)} %bitcast.57), channel_id=1, source_target_pairs={{0,1},{1,2},{2,3},{4,5},{5,6},{6,7},{8,9},{9,10},{10,11},{12,13},{... | collective-permute-start | bytes 786440 | tf_op jit(solution)/shard_map/ppermute | solution.py:17
  133.8 5.3 %collective-permute-done.15 = f32[8,1,32,128]{3,2,1,0:T(8,128)S(1)} collective-permute-done((f32[8,1,32,128]{3,2,1,0:T(8,128)S(1)}, f32[8,1,32,128]{3,2,1,0:T(8,128)S(1)}, u32[]{:S(2)}, u32[]{:S(2)}) %collective-permute-start.15) | collective-permute-done | bytes 131104 | tf_op jit(solution)/shard_map/ppermute | solution.py:18
  139.1 23.8 %fusion.38 = f32[8,64,32,128]{3,2,1,0:T(8,128)} fusion(f32[8,64,32,128]{3,2,1,0:T(8,128)} %fusion.49, f32[8,64,1,128]{3,2,1,0:T(1,128)S(1)} %bitcast.44, f32[10,1,32,128]{3,2,1,0:T(8,128)S(1)} %pad.83, f32[10,1,32,128]{3,2,1,0:T(8,128)S(1)} %pad.82, f32[1,64,32,128]{3,2,1,0:T(8,128)S(1)} %collective-permute-done.13, ...), kind=kLoop, calls=%fused_computation.94 | loop fusion | flops 79691776 | bytes 28114944 | tf_op jit(solution)/shard_map/add | solution.py:57
  162.9 1.7 fusion.73
  165.9 7.2 %collective-permute-start.19 = (f32[1,64,32,128]{3,2,1,0:T(8,128)S(1)}, f32[1,64,32,128]{3,2,1,0:T(8,128)S(1)}, u32[]{:S(2)}, u32[]{:S(2)}) collective-permute-start(f32[1,64,32,128]{3,2,1,0:T(8,128)S(1)} %get-tuple-element.63), channel_id=1, source_target_pairs={{32,0},{64,32},{96,64},{33,1},{65,33},{97,65},{34,2},{66,34},{98,6... | collective-permute-start | bytes 3145736 | tf_op jit(solution)/shard_map/ppermute | solution.py:18
  174.1 5.8 %collective-permute-start.20 = (f32[8,1,32,128]{3,2,1,0:T(8,128)S(1)}, f32[8,1,32,128]{3,2,1,0:T(8,128)S(1)}, u32[]{:S(2)}, u32[]{:S(2)}) collective-permute-start(f32[8,1,32,128]{3,2,1,0:T(8,128)S(1)} %get-tuple-element.64), channel_id=1, source_target_pairs={{0,4},{4,8},{8,12},{12,16},{16,20},{20,24},{24,28},{1,5},{5,9},{9,... | collective-permute-start | bytes 393224 | tf_op jit(solution)/shard_map/ppermute | solution.py:17
  179.9 2.6 fusion.72
  182.6 4.3 %collective-permute-start.22 = (f32[8,64,1,128]{3,1,2,0:T(8,128)S(1)}, f32[8,64,1,128]{3,1,2,0:T(8,128)S(1)}, u32[]{:S(2)}, u32[]{:S(2)}) collective-permute-start(f32[8,64,1,128]{3,1,2,0:T(8,128)S(1)} %bitcast.58), channel_id=1, source_target_pairs={{0,1},{1,2},{2,3},{4,5},{5,6},{6,7},{8,9},{9,10},{10,11},{12,13},{... | collective-permute-start | bytes 786440 | tf_op jit(solution)/shard_map/ppermute | solution.py:17
  189.5 4.7 %collective-permute-done.21 = f32[8,1,32,128]{3,2,1,0:T(8,128)S(1)} collective-permute-done((f32[8,1,32,128]{3,2,1,0:T(8,128)S(1)}, f32[8,1,32,128]{3,2,1,0:T(8,128)S(1)}, u32[]{:S(2)}, u32[]{:S(2)}) %collective-permute-start.21) | collective-permute-done | bytes 131104 | tf_op jit(solution)/shard_map/ppermute | solution.py:18
  194.2 23.7 %fusion.27 = f32[8,64,32,128]{3,2,1,0:T(8,128)} fusion(f32[8,64,32,128]{3,2,1,0:T(8,128)} %fusion.38, f32[8,64,1,128]{3,2,1,0:T(1,128)S(1)} %bitcast.45, f32[10,1,32,128]{3,2,1,0:T(8,128)S(1)} %pad.87, f32[10,1,32,128]{3,2,1,0:T(8,128)S(1)} %pad.86, f32[1,64,32,128]{3,2,1,0:T(8,128)S(1)} %collective-permute-done.19, ...), kind=kLoop, calls=%fused_computation.65 | loop fusion | flops 79691776 | bytes 28114944 | tf_op jit(solution)/shard_map/add | solution.py:57
  217.9 1.7 fusion.70
  221.0 7.2 %collective-permute-start.25 = (f32[1,64,32,128]{3,2,1,0:T(8,128)S(1)}, f32[1,64,32,128]{3,2,1,0:T(8,128)S(1)}, u32[]{:S(2)}, u32[]{:S(2)}) collective-permute-start(f32[1,64,32,128]{3,2,1,0:T(8,128)S(1)} %get-tuple-element.57), channel_id=1, source_target_pairs={{32,0},{64,32},{96,64},{33,1},{65,33},{97,65},{34,2},{66,34},{98,6... | collective-permute-start | bytes 3145736 | tf_op jit(solution)/shard_map/ppermute | solution.py:18
  229.2 3.7 collective-permute-start.26
  232.9 2.6 fusion.69
  235.6 4.3 %collective-permute-start.28 = (f32[8,64,1,128]{3,1,2,0:T(8,128)S(1)}, f32[8,64,1,128]{3,1,2,0:T(8,128)S(1)}, u32[]{:S(2)}, u32[]{:S(2)}) collective-permute-start(f32[8,64,1,128]{3,1,2,0:T(8,128)S(1)} %bitcast.59), channel_id=1, source_target_pairs={{0,1},{1,2},{2,3},{4,5},{5,6},{6,7},{8,9},{9,10},{10,11},{12,13},{... | collective-permute-start | bytes 786440 | tf_op jit(solution)/shard_map/ppermute | solution.py:17
  242.5 4.7 %collective-permute-done.27 = f32[8,1,32,128]{3,2,1,0:T(8,128)S(1)} collective-permute-done((f32[8,1,32,128]{3,2,1,0:T(8,128)S(1)}, f32[8,1,32,128]{3,2,1,0:T(8,128)S(1)}, u32[]{:S(2)}, u32[]{:S(2)}) %collective-permute-start.27) | collective-permute-done | bytes 131104 | tf_op jit(solution)/shard_map/ppermute | solution.py:18
  247.2 23.8 %fusion.16 = f32[8,64,32,128]{3,2,1,0:T(8,128)} fusion(f32[8,64,32,128]{3,2,1,0:T(8,128)} %fusion.27, f32[8,64,1,128]{3,2,1,0:T(1,128)S(1)} %bitcast.46, f32[10,1,32,128]{3,2,1,0:T(8,128)S(1)} %pad.91, f32[10,1,32,128]{3,2,1,0:T(8,128)S(1)} %pad.90, f32[1,64,32,128]{3,2,1,0:T(8,128)S(1)} %collective-permute-done.25, ...), kind=kLoop, calls=%fused_computation.36 | loop fusion | flops 79691776 | bytes 28114944 | tf_op jit(solution)/shard_map/add | solution.py:57
  271.0 1.7 fusion.67
  274.0 7.2 %collective-permute-start.31 = (f32[1,64,32,128]{3,2,1,0:T(8,128)S(1)}, f32[1,64,32,128]{3,2,1,0:T(8,128)S(1)}, u32[]{:S(2)}, u32[]{:S(2)}) collective-permute-start(f32[1,64,32,128]{3,2,1,0:T(8,128)S(1)} %get-tuple-element.51), channel_id=1, source_target_pairs={{32,0},{64,32},{96,64},{33,1},{65,33},{97,65},{34,2},{66,34},{98,6... | collective-permute-start | bytes 3145736 | tf_op jit(solution)/shard_map/ppermute | solution.py:18
  282.3 3.7 collective-permute-start.32
  286.0 2.6 fusion.66
  288.7 4.3 %collective-permute-start.34 = (f32[8,64,1,128]{3,1,2,0:T(8,128)S(1)}, f32[8,64,1,128]{3,1,2,0:T(8,128)S(1)}, u32[]{:S(2)}, u32[]{:S(2)}) collective-permute-start(f32[8,64,1,128]{3,1,2,0:T(8,128)S(1)} %bitcast.60), channel_id=1, source_target_pairs={{0,1},{1,2},{2,3},{4,5},{5,6},{6,7},{8,9},{9,10},{10,11},{12,13},{... | collective-permute-start | bytes 786440 | tf_op jit(solution)/shard_map/ppermute | solution.py:17
  295.8 4.4 %collective-permute-done.33 = f32[8,1,32,128]{3,2,1,0:T(8,128)S(1)} collective-permute-done((f32[8,1,32,128]{3,2,1,0:T(8,128)S(1)}, f32[8,1,32,128]{3,2,1,0:T(8,128)S(1)}, u32[]{:S(2)}, u32[]{:S(2)}) %collective-permute-start.33) | collective-permute-done | bytes 131104 | tf_op jit(solution)/shard_map/ppermute | solution.py:18
  300.3 23.7 %fusion.5 = f32[8,64,32,128]{3,2,1,0:T(8,128)} fusion(f32[8,64,32,128]{3,2,1,0:T(8,128)} %fusion.16, f32[8,64,1,128]{3,2,1,0:T(1,128)S(1)} %bitcast.47, f32[10,1,32,128]{3,2,1,0:T(8,128)S(1)} %pad.95, f32[10,1,32,128]{3,2,1,0:T(8,128)S(1)} %pad.94, f32[1,64,32,128]{3,2,1,0:T(8,128)S(1)} %collective-permute-done.31, ...), kind=kLoop, calls=%fused_computation.7 | loop fusion | flops 79691776 | bytes 28114944 | tf_op jit(solution)/shard_map/add | solution.py:57
  324.0 7.9 %fusion.84 = f32[8,64,32,128]{3,2,1,0:T(8,128)} fusion(f32[8,64,32,128]{3,2,1,0:T(8,128)} %fusion.5), kind=kOutput, calls=%fused_computation.191 | output fusion | flops 14680064 | bytes 16777216 | tf_op jit(solution)/shard_map/jit(cumsum)/reduce_window_sum | solution.py:64
  331.9 2.3 slice.556
  334.3 44.5 %all-gather.3.cloned.1.call-done = f32[4,64,32,128]{3,2,1,0:T(8,128)} async-done(((f32[1,64,32,128]{3,2,1,0:T(8,128)}), f32[4,64,32,128]{3,2,1,0:T(8,128)}) %all-gather.3.cloned.1.call-update) | async-done | bytes 4194320 | tf_op jit(solution)/shard_map/all_gather | solution.py:31
  378.8 4.6 %while.10 = (s32[]{:T(128)}, f32[1,64,32,128]{3,2,1,0:T(8,128)S(1)}, s32[]{:T(128)}, f32[4,1,64,32,128]{4,3,2,1,0:T(8,128)}, s32[]{:T(128)}, /*index=5*/s32[]{:T(128)}, s32[]{:T(128)}) while((s32[]{:T(128)}, f32[1,64,32,128]{3,2,1,0:T(8,128)S(1)}, s32[]{:T(128)}, f32[4,1,64,32,128]{4,3,2,1,0:T(8,128)}, s32[]{:T(128)}, /*index=5*/s32[]{:T(128)}, ...), condition=%wide.region_2.3_spmd, body=%wide.region_1.2_spmd.sunk | while | flops 262149 | bytes 3145843 | solution.py:37
  383.4 8.5 %add_multiply_fusion = f32[8,64,32,128]{3,2,1,0:T(8,128)} fusion(f32[8,64,32,128]{3,2,1,0:T(8,128)} %fusion.84, f32[64,32,128]{2,1,0:T(8,128)S(1)} %bitcast.35), kind=kLoop, calls=%fused_computation.169 | loop fusion | flops 4194304 | bytes 17825792 | tf_op jit(solution)/shard_map/div | solution.py:71
  (81 shorter events, 35.5 us)
Async XLA Ops:
  7.2 371.5 %all-gather.3.cloned.1.call-start = ((), (), s32[]{:S(2)}) async-start(), calls=%async_computation | async-start | bytes 5242880 | tf_op jit(solution)/shard_map/all_gather | solution.py:31
  7.2 20.5 %copy-start = (f32[8,64,32,128]{3,2,1,0:T(8,128)S(1)}, f32[8,64,32,128]{3,2,1,0:T(8,128)}, u32[]{:S(2)}) copy-start(f32[8,64,32,128]{3,2,1,0:T(8,128)} %param.4) | copy-start | bytes 25165828
  9.1 17.5 %collective-permute-start = (f32[1,64,32,128]{3,2,1,0:T(8,128)S(1)}, f32[1,64,32,128]{3,2,1,0:T(8,128)S(1)}, u32[]{:S(2)}, u32[]{:S(2)}) collective-permute-start(f32[1,64,32,128]{3,2,1,0:T(8,128)S(1)} %get-tuple-element.83), channel_id=1, source_target_pairs={{0,32},{32,64},{64,96},{1,33},{33,65},{65,97},{2,34},{34,66},{66,9... | collective-permute-start | bytes 3145736 | tf_op jit(solution)/shard_map/ppermute | solution.py:17
  10.7 21.7 %collective-permute-start.1 = (f32[1,64,32,128]{3,2,1,0:T(8,128)S(1)}, f32[1,64,32,128]{3,2,1,0:T(8,128)S(1)}, u32[]{:S(2)}, u32[]{:S(2)}) collective-permute-start(f32[1,64,32,128]{3,2,1,0:T(8,128)S(1)} %get-tuple-element.82), channel_id=1, source_target_pairs={{32,0},{64,32},{96,64},{33,1},{65,33},{97,65},{34,2},{66,34},{98,6... | collective-permute-start | bytes 3145736 | tf_op jit(solution)/shard_map/ppermute | solution.py:18
  14.9 10.3 %collective-permute-start.2 = (f32[8,1,32,128]{3,2,1,0:T(8,128)S(1)}, f32[8,1,32,128]{3,2,1,0:T(8,128)S(1)}, u32[]{:S(2)}, u32[]{:S(2)}) collective-permute-start(f32[8,1,32,128]{3,2,1,0:T(8,128)S(1)} %get-tuple-element.80), channel_id=1, source_target_pairs={{0,4},{4,8},{8,12},{12,16},{16,20},{20,24},{24,28},{1,5},{5,9},{9,... | collective-permute-start | bytes 393224 | tf_op jit(solution)/shard_map/ppermute | solution.py:17
  18.1 8.5 %collective-permute-start.3 = (f32[8,1,32,128]{3,2,1,0:T(8,128)S(1)}, f32[8,1,32,128]{3,2,1,0:T(8,128)S(1)}, u32[]{:S(2)}, u32[]{:S(2)}) collective-permute-start(f32[8,1,32,128]{3,2,1,0:T(8,128)S(1)} %get-tuple-element.81), channel_id=1, source_target_pairs={{4,0},{8,4},{12,8},{16,12},{20,16},{24,20},{28,24},{5,1},{9,5},{13... | collective-permute-start | bytes 393224 | tf_op jit(solution)/shard_map/ppermute | solution.py:18
  22.0 11.4 %collective-permute-start.4 = (f32[8,64,1,128]{3,1,2,0:T(8,128)S(1)}, f32[8,64,1,128]{3,1,2,0:T(8,128)S(1)}, u32[]{:S(2)}, u32[]{:S(2)}) collective-permute-start(f32[8,64,1,128]{3,1,2,0:T(8,128)S(1)} %bitcast.50), channel_id=1, source_target_pairs={{0,1},{1,2},{2,3},{4,5},{5,6},{6,7},{8,9},{9,10},{10,11},{12,13},{... | collective-permute-start | bytes 786440 | tf_op jit(solution)/shard_map/ppermute | solution.py:17
  25.3 8.1 %collective-permute-start.5 = (f32[8,64,1,128]{3,1,2,0:T(8,128)S(1)}, f32[8,64,1,128]{3,1,2,0:T(8,128)S(1)}, u32[]{:S(2)}, u32[]{:S(2)}) collective-permute-start(f32[8,64,1,128]{3,1,2,0:T(8,128)S(1)} %bitcast.49), channel_id=1, source_target_pairs={{1,0},{2,1},{3,2},{5,4},{6,5},{7,6},{9,8},{10,9},{11,10},{13,12},{... | collective-permute-start | bytes 786440 | tf_op jit(solution)/shard_map/ppermute | solution.py:18
  26.6 6.8 %slice-start = ((s8[8388608]{0:T(1024)(128)(4,1)}), s8[4194304]{0:T(1024)(128)(4,1)S(1)}, s32[]{:S(2)}) async-start(s8[8388608]{0:T(1024)(128)(4,1)} %bitcast.33), calls=%async_computation.1 | async-start | bytes 8388608
  27.7 5.7 %slice-start.1 = ((s8[8388608]{0:T(1024)(128)(4,1)}), s8[4194304]{0:T(1024)(128)(4,1)S(1)}, s32[]{:S(2)}) async-start(s8[8388608]{0:T(1024)(128)(4,1)} %bitcast.33), calls=%async_computation.2 | async-start | bytes 8388608
  58.7 27.0 %collective-permute-start.6 = (f32[1,64,32,128]{3,2,1,0:T(8,128)S(1)}, f32[1,64,32,128]{3,2,1,0:T(8,128)S(1)}, u32[]{:S(2)}, u32[]{:S(2)}) collective-permute-start(f32[1,64,32,128]{3,2,1,0:T(8,128)S(1)} %get-tuple-element.74), channel_id=1, source_target_pairs={{0,32},{32,64},{64,96},{1,33},{33,65},{65,97},{2,34},{34,66},{66,9... | collective-permute-start | bytes 3145736 | tf_op jit(solution)/shard_map/ppermute | solution.py:17
  60.0 25.7 %collective-permute-start.7 = (f32[1,64,32,128]{3,2,1,0:T(8,128)S(1)}, f32[1,64,32,128]{3,2,1,0:T(8,128)S(1)}, u32[]{:S(2)}, u32[]{:S(2)}) collective-permute-start(f32[1,64,32,128]{3,2,1,0:T(8,128)S(1)} %get-tuple-element.75), channel_id=1, source_target_pairs={{32,0},{64,32},{96,64},{33,1},{65,33},{97,65},{34,2},{66,34},{98,6... | collective-permute-start | bytes 3145736 | tf_op jit(solution)/shard_map/ppermute | solution.py:18
  67.5 12.4 %collective-permute-start.8 = (f32[8,1,32,128]{3,2,1,0:T(8,128)S(1)}, f32[8,1,32,128]{3,2,1,0:T(8,128)S(1)}, u32[]{:S(2)}, u32[]{:S(2)}) collective-permute-start(f32[8,1,32,128]{3,2,1,0:T(8,128)S(1)} %get-tuple-element.76), channel_id=1, source_target_pairs={{0,4},{4,8},{8,12},{12,16},{16,20},{20,24},{24,28},{1,5},{5,9},{9,... | collective-permute-start | bytes 393224 | tf_op jit(solution)/shard_map/ppermute | solution.py:17
  74.4 11.2 %collective-permute-start.10 = (f32[8,64,1,128]{3,1,2,0:T(8,128)S(1)}, f32[8,64,1,128]{3,1,2,0:T(8,128)S(1)}, u32[]{:S(2)}, u32[]{:S(2)}) collective-permute-start(f32[8,64,1,128]{3,1,2,0:T(8,128)S(1)} %bitcast.56), channel_id=1, source_target_pairs={{0,1},{1,2},{2,3},{4,5},{5,6},{6,7},{8,9},{9,10},{10,11},{12,13},{... | collective-permute-start | bytes 786440 | tf_op jit(solution)/shard_map/ppermute | solution.py:17
  78.6 7.1 %collective-permute-start.11 = (f32[8,64,1,128]{3,1,2,0:T(8,128)S(1)}, f32[8,64,1,128]{3,1,2,0:T(8,128)S(1)}, u32[]{:S(2)}, u32[]{:S(2)}) collective-permute-start(f32[8,64,1,128]{3,1,2,0:T(8,128)S(1)} %bitcast.51), channel_id=1, source_target_pairs={{1,0},{2,1},{3,2},{5,4},{6,5},{7,6},{9,8},{10,9},{11,10},{13,12},{... | collective-permute-start | bytes 786440 | tf_op jit(solution)/shard_map/ppermute | solution.py:18
  79.9 5.7 %collective-permute-start.9 = (f32[8,1,32,128]{3,2,1,0:T(8,128)S(1)}, f32[8,1,32,128]{3,2,1,0:T(8,128)S(1)}, u32[]{:S(2)}, u32[]{:S(2)}) collective-permute-start(f32[8,1,32,128]{3,2,1,0:T(8,128)S(1)} %get-tuple-element.77), channel_id=1, source_target_pairs={{4,0},{8,4},{12,8},{16,12},{20,16},{24,20},{28,24},{5,1},{9,5},{13... | collective-permute-start | bytes 393224 | tf_op jit(solution)/shard_map/ppermute | solution.py:18
  111.1 28.0 %collective-permute-start.12 = (f32[1,64,32,128]{3,2,1,0:T(8,128)S(1)}, f32[1,64,32,128]{3,2,1,0:T(8,128)S(1)}, u32[]{:S(2)}, u32[]{:S(2)}) collective-permute-start(f32[1,64,32,128]{3,2,1,0:T(8,128)S(1)} %get-tuple-element.68), channel_id=1, source_target_pairs={{0,32},{32,64},{64,96},{1,33},{33,65},{65,97},{2,34},{34,66},{66,9... | collective-permute-start | bytes 3145736 | tf_op jit(solution)/shard_map/ppermute | solution.py:17
  112.4 26.7 %collective-permute-start.13 = (f32[1,64,32,128]{3,2,1,0:T(8,128)S(1)}, f32[1,64,32,128]{3,2,1,0:T(8,128)S(1)}, u32[]{:S(2)}, u32[]{:S(2)}) collective-permute-start(f32[1,64,32,128]{3,2,1,0:T(8,128)S(1)} %get-tuple-element.69), channel_id=1, source_target_pairs={{32,0},{64,32},{96,64},{33,1},{65,33},{97,65},{34,2},{66,34},{98,6... | collective-permute-start | bytes 3145736 | tf_op jit(solution)/shard_map/ppermute | solution.py:18
  120.9 11.3 %collective-permute-start.14 = (f32[8,1,32,128]{3,2,1,0:T(8,128)S(1)}, f32[8,1,32,128]{3,2,1,0:T(8,128)S(1)}, u32[]{:S(2)}, u32[]{:S(2)}) collective-permute-start(f32[8,1,32,128]{3,2,1,0:T(8,128)S(1)} %get-tuple-element.70), channel_id=1, source_target_pairs={{0,4},{4,8},{8,12},{12,16},{16,20},{20,24},{24,28},{1,5},{5,9},{9,... | collective-permute-start | bytes 393224 | tf_op jit(solution)/shard_map/ppermute | solution.py:17
  126.7 12.4 %collective-permute-start.16 = (f32[8,64,1,128]{3,1,2,0:T(8,128)S(1)}, f32[8,64,1,128]{3,1,2,0:T(8,128)S(1)}, u32[]{:S(2)}, u32[]{:S(2)}) collective-permute-start(f32[8,64,1,128]{3,1,2,0:T(8,128)S(1)} %bitcast.57), channel_id=1, source_target_pairs={{0,1},{1,2},{2,3},{4,5},{5,6},{6,7},{8,9},{9,10},{10,11},{12,13},{... | collective-permute-start | bytes 786440 | tf_op jit(solution)/shard_map/ppermute | solution.py:17
  131.0 8.1 %collective-permute-start.17 = (f32[8,64,1,128]{3,1,2,0:T(8,128)S(1)}, f32[8,64,1,128]{3,1,2,0:T(8,128)S(1)}, u32[]{:S(2)}, u32[]{:S(2)}) collective-permute-start(f32[8,64,1,128]{3,1,2,0:T(8,128)S(1)} %bitcast.52), channel_id=1, source_target_pairs={{1,0},{2,1},{3,2},{5,4},{6,5},{7,6},{9,8},{10,9},{11,10},{13,12},{... | collective-permute-start | bytes 786440 | tf_op jit(solution)/shard_map/ppermute | solution.py:18
  132.3 6.8 %collective-permute-start.15 = (f32[8,1,32,128]{3,2,1,0:T(8,128)S(1)}, f32[8,1,32,128]{3,2,1,0:T(8,128)S(1)}, u32[]{:S(2)}, u32[]{:S(2)}) collective-permute-start(f32[8,1,32,128]{3,2,1,0:T(8,128)S(1)} %get-tuple-element.71), channel_id=1, source_target_pairs={{4,0},{8,4},{12,8},{16,12},{20,16},{24,20},{28,24},{5,1},{9,5},{13... | collective-permute-start | bytes 393224 | tf_op jit(solution)/shard_map/ppermute | solution.py:18
  164.6 29.6 %collective-permute-start.18 = (f32[1,64,32,128]{3,2,1,0:T(8,128)S(1)}, f32[1,64,32,128]{3,2,1,0:T(8,128)S(1)}, u32[]{:S(2)}, u32[]{:S(2)}) collective-permute-start(f32[1,64,32,128]{3,2,1,0:T(8,128)S(1)} %get-tuple-element.62), channel_id=1, source_target_pairs={{0,32},{32,64},{64,96},{1,33},{33,65},{65,97},{2,34},{34,66},{66,9... | collective-permute-start | bytes 3145736 | tf_op jit(solution)/shard_map/ppermute | solution.py:17
  165.9 28.3 %collective-permute-start.19 = (f32[1,64,32,128]{3,2,1,0:T(8,128)S(1)}, f32[1,64,32,128]{3,2,1,0:T(8,128)S(1)}, u32[]{:S(2)}, u32[]{:S(2)}) collective-permute-start(f32[1,64,32,128]{3,2,1,0:T(8,128)S(1)} %get-tuple-element.63), channel_id=1, source_target_pairs={{32,0},{64,32},{96,64},{33,1},{65,33},{97,65},{34,2},{66,34},{98,6... | collective-permute-start | bytes 3145736 | tf_op jit(solution)/shard_map/ppermute | solution.py:18
  174.1 14.0 %collective-permute-start.20 = (f32[8,1,32,128]{3,2,1,0:T(8,128)S(1)}, f32[8,1,32,128]{3,2,1,0:T(8,128)S(1)}, u32[]{:S(2)}, u32[]{:S(2)}) collective-permute-start(f32[8,1,32,128]{3,2,1,0:T(8,128)S(1)} %get-tuple-element.64), channel_id=1, source_target_pairs={{0,4},{4,8},{8,12},{12,16},{16,20},{20,24},{24,28},{1,5},{5,9},{9,... | collective-permute-start | bytes 393224 | tf_op jit(solution)/shard_map/ppermute | solution.py:17
  182.6 11.6 %collective-permute-start.22 = (f32[8,64,1,128]{3,1,2,0:T(8,128)S(1)}, f32[8,64,1,128]{3,1,2,0:T(8,128)S(1)}, u32[]{:S(2)}, u32[]{:S(2)}) collective-permute-start(f32[8,64,1,128]{3,1,2,0:T(8,128)S(1)} %bitcast.58), channel_id=1, source_target_pairs={{0,1},{1,2},{2,3},{4,5},{5,6},{6,7},{8,9},{9,10},{10,11},{12,13},{... | collective-permute-start | bytes 786440 | tf_op jit(solution)/shard_map/ppermute | solution.py:17
  186.9 7.3 %collective-permute-start.23 = (f32[8,64,1,128]{3,1,2,0:T(8,128)S(1)}, f32[8,64,1,128]{3,1,2,0:T(8,128)S(1)}, u32[]{:S(2)}, u32[]{:S(2)}) collective-permute-start(f32[8,64,1,128]{3,1,2,0:T(8,128)S(1)} %bitcast.53), channel_id=1, source_target_pairs={{1,0},{2,1},{3,2},{5,4},{6,5},{7,6},{9,8},{10,9},{11,10},{13,12},{... | collective-permute-start | bytes 786440 | tf_op jit(solution)/shard_map/ppermute | solution.py:18
  188.2 6.0 %collective-permute-start.21 = (f32[8,1,32,128]{3,2,1,0:T(8,128)S(1)}, f32[8,1,32,128]{3,2,1,0:T(8,128)S(1)}, u32[]{:S(2)}, u32[]{:S(2)}) collective-permute-start(f32[8,1,32,128]{3,2,1,0:T(8,128)S(1)} %get-tuple-element.65), channel_id=1, source_target_pairs={{4,0},{8,4},{12,8},{16,12},{20,16},{24,20},{28,24},{5,1},{9,5},{13... | collective-permute-start | bytes 393224 | tf_op jit(solution)/shard_map/ppermute | solution.py:18
  219.7 27.6 %collective-permute-start.24 = (f32[1,64,32,128]{3,2,1,0:T(8,128)S(1)}, f32[1,64,32,128]{3,2,1,0:T(8,128)S(1)}, u32[]{:S(2)}, u32[]{:S(2)}) collective-permute-start(f32[1,64,32,128]{3,2,1,0:T(8,128)S(1)} %get-tuple-element.56), channel_id=1, source_target_pairs={{0,32},{32,64},{64,96},{1,33},{33,65},{65,97},{2,34},{34,66},{66,9... | collective-permute-start | bytes 3145736 | tf_op jit(solution)/shard_map/ppermute | solution.py:17
  221.0 26.3 %collective-permute-start.25 = (f32[1,64,32,128]{3,2,1,0:T(8,128)S(1)}, f32[1,64,32,128]{3,2,1,0:T(8,128)S(1)}, u32[]{:S(2)}, u32[]{:S(2)}) collective-permute-start(f32[1,64,32,128]{3,2,1,0:T(8,128)S(1)} %get-tuple-element.57), channel_id=1, source_target_pairs={{32,0},{64,32},{96,64},{33,1},{65,33},{97,65},{34,2},{66,34},{98,6... | collective-permute-start | bytes 3145736 | tf_op jit(solution)/shard_map/ppermute | solution.py:18
  229.2 12.0 %collective-permute-start.26 = (f32[8,1,32,128]{3,2,1,0:T(8,128)S(1)}, f32[8,1,32,128]{3,2,1,0:T(8,128)S(1)}, u32[]{:S(2)}, u32[]{:S(2)}) collective-permute-start(f32[8,1,32,128]{3,2,1,0:T(8,128)S(1)} %get-tuple-element.58), channel_id=1, source_target_pairs={{0,4},{4,8},{8,12},{12,16},{16,20},{20,24},{24,28},{1,5},{5,9},{9,... | collective-permute-start | bytes 393224 | tf_op jit(solution)/shard_map/ppermute | solution.py:17
  235.6 11.6 %collective-permute-start.28 = (f32[8,64,1,128]{3,1,2,0:T(8,128)S(1)}, f32[8,64,1,128]{3,1,2,0:T(8,128)S(1)}, u32[]{:S(2)}, u32[]{:S(2)}) collective-permute-start(f32[8,64,1,128]{3,1,2,0:T(8,128)S(1)} %bitcast.59), channel_id=1, source_target_pairs={{0,1},{1,2},{2,3},{4,5},{5,6},{6,7},{8,9},{9,10},{10,11},{12,13},{... | collective-permute-start | bytes 786440 | tf_op jit(solution)/shard_map/ppermute | solution.py:17
  239.9 7.3 %collective-permute-start.29 = (f32[8,64,1,128]{3,1,2,0:T(8,128)S(1)}, f32[8,64,1,128]{3,1,2,0:T(8,128)S(1)}, u32[]{:S(2)}, u32[]{:S(2)}) collective-permute-start(f32[8,64,1,128]{3,1,2,0:T(8,128)S(1)} %bitcast.54), channel_id=1, source_target_pairs={{1,0},{2,1},{3,2},{5,4},{6,5},{7,6},{9,8},{10,9},{11,10},{13,12},{... | collective-permute-start | bytes 786440 | tf_op jit(solution)/shard_map/ppermute | solution.py:18
  241.2 6.0 %collective-permute-start.27 = (f32[8,1,32,128]{3,2,1,0:T(8,128)S(1)}, f32[8,1,32,128]{3,2,1,0:T(8,128)S(1)}, u32[]{:S(2)}, u32[]{:S(2)}) collective-permute-start(f32[8,1,32,128]{3,2,1,0:T(8,128)S(1)} %get-tuple-element.59), channel_id=1, source_target_pairs={{4,0},{8,4},{12,8},{16,12},{20,16},{24,20},{28,24},{5,1},{9,5},{13... | collective-permute-start | bytes 393224 | tf_op jit(solution)/shard_map/ppermute | solution.py:18
  272.7 27.6 %collective-permute-start.30 = (f32[1,64,32,128]{3,2,1,0:T(8,128)S(1)}, f32[1,64,32,128]{3,2,1,0:T(8,128)S(1)}, u32[]{:S(2)}, u32[]{:S(2)}) collective-permute-start(f32[1,64,32,128]{3,2,1,0:T(8,128)S(1)} %get-tuple-element.50), channel_id=1, source_target_pairs={{0,32},{32,64},{64,96},{1,33},{33,65},{65,97},{2,34},{34,66},{66,9... | collective-permute-start | bytes 3145736 | tf_op jit(solution)/shard_map/ppermute | solution.py:17
  274.0 26.3 %collective-permute-start.31 = (f32[1,64,32,128]{3,2,1,0:T(8,128)S(1)}, f32[1,64,32,128]{3,2,1,0:T(8,128)S(1)}, u32[]{:S(2)}, u32[]{:S(2)}) collective-permute-start(f32[1,64,32,128]{3,2,1,0:T(8,128)S(1)} %get-tuple-element.51), channel_id=1, source_target_pairs={{32,0},{64,32},{96,64},{33,1},{65,33},{97,65},{34,2},{66,34},{98,6... | collective-permute-start | bytes 3145736 | tf_op jit(solution)/shard_map/ppermute | solution.py:18
  282.3 12.0 %collective-permute-start.32 = (f32[8,1,32,128]{3,2,1,0:T(8,128)S(1)}, f32[8,1,32,128]{3,2,1,0:T(8,128)S(1)}, u32[]{:S(2)}, u32[]{:S(2)}) collective-permute-start(f32[8,1,32,128]{3,2,1,0:T(8,128)S(1)} %get-tuple-element.52), channel_id=1, source_target_pairs={{0,4},{4,8},{8,12},{12,16},{16,20},{20,24},{24,28},{1,5},{5,9},{9,... | collective-permute-start | bytes 393224 | tf_op jit(solution)/shard_map/ppermute | solution.py:17
  288.7 11.6 %collective-permute-start.34 = (f32[8,64,1,128]{3,1,2,0:T(8,128)S(1)}, f32[8,64,1,128]{3,1,2,0:T(8,128)S(1)}, u32[]{:S(2)}, u32[]{:S(2)}) collective-permute-start(f32[8,64,1,128]{3,1,2,0:T(8,128)S(1)} %bitcast.60), channel_id=1, source_target_pairs={{0,1},{1,2},{2,3},{4,5},{5,6},{6,7},{8,9},{9,10},{10,11},{12,13},{... | collective-permute-start | bytes 786440 | tf_op jit(solution)/shard_map/ppermute | solution.py:17
  292.9 7.3 %collective-permute-start.35 = (f32[8,64,1,128]{3,1,2,0:T(8,128)S(1)}, f32[8,64,1,128]{3,1,2,0:T(8,128)S(1)}, u32[]{:S(2)}, u32[]{:S(2)}) collective-permute-start(f32[8,64,1,128]{3,1,2,0:T(8,128)S(1)} %bitcast.55), channel_id=1, source_target_pairs={{1,0},{2,1},{3,2},{5,4},{6,5},{7,6},{9,8},{10,9},{11,10},{13,12},{... | collective-permute-start | bytes 786440 | tf_op jit(solution)/shard_map/ppermute | solution.py:18
  294.3 6.0 %collective-permute-start.33 = (f32[8,1,32,128]{3,2,1,0:T(8,128)S(1)}, f32[8,1,32,128]{3,2,1,0:T(8,128)S(1)}, u32[]{:S(2)}, u32[]{:S(2)}) collective-permute-start(f32[8,1,32,128]{3,2,1,0:T(8,128)S(1)} %get-tuple-element.53), channel_id=1, source_target_pairs={{4,0},{8,4},{12,8},{16,12},{20,16},{24,20},{28,24},{5,1},{9,5},{13... | collective-permute-start | bytes 393224 | tf_op jit(solution)/shard_map/ppermute | solution.py:18
Sparse Core Ops, SparseCore 0:
  334.4 44.2 all-gather.2
where the time goes:
time: 402 us; the launch traced here: 399 us
  other arithmetic  163 us (41%)
  starting transfers between devices  111 us (28%)
  waiting for transfers between devices  68.1 us (17%)
  local copies, waits for them, and re-layouts  41.6 us (10%)
  between operations  14.7 us (4%)
    add x6, other arithmetic, march_step(): return middle + 0.1 * spread + 0.2 * middle * (1.0 - middle * crowding)  142 us
    ppermute x18, starting transfers between devices, with_halo(): lax.ppermute(last, axis, up)  56.2 us
    ppermute x18, starting transfers between devices, with_halo(): lax.ppermute(leading, axis, [(b, a) for a, b in up])  54.8 us
    all_gather x1, waiting for transfers between devices, entering(): gathered = lax.all_gather(part, axis)  44.5 us
    slice x17, local copies, waits for them, and re-layouts, with_halo(): last = lax.slice_in_dim(array, length - width, length, axis=dim)  30.4 us
    ppermute x18, waiting for transfers between devices, with_halo(): lax.ppermute(leading, axis, [(b, a) for a, b in up])  23.6 us
    div x1, other arithmetic, local(): column_sum = (here + below) / (density.shape[0] * lax.axis_size('py'))  8.49 us
  transfers between devices with their start and end apart: 37, of which 7 were waited for; matrix products, arithmetic and copies ran while one was open for 7% of the time, Pallas kernels for 0%

commit v1 on v0

v1 whole, which is shorter than its diff:
```python
import functools

import jax
import jax.numpy as jnp
from jax import lax
from jax.experimental import pallas as pl
from jax.experimental.pallas import tpu as pltpu
from jax.sharding import PartitionSpec as P

STEPS = 6
CHUNKS = 8
MESH = pl.DeviceIdType.MESH
LOW, HIGH = 8, 40


def kernel(sizes, d_ref, c_ref, col_ref, end_ref, field, crowd, below, total,
           in_sem, c_sem, y_send, y_recv, z_send, z_recv, x_send, x_recv, t_send, t_recv):
    ny, nx, nz = sizes
    py, px, pz = lax.axis_index("py"), lax.axis_index("px"), lax.axis_index("pz")
    Y, X, Z, _ = d_ref.shape
    width = X // CHUNKS
    even = lax.rem(px, 2) == 0

    def start_of(k):
        return pl.multiple_of(jnp.where(even, k, CHUNKS - 1 - k) * width, width)

    y_up = (py < ny - 1, {"py": py + 1, "px": px, "pz": pz})
    y_down = (py > 0, {"py": py - 1, "px": px, "pz": pz})
    z_up = (pz < nz - 1, {"py": py, "px": px, "pz": pz + 1})
    z_down = (pz > 0, {"py": py, "px": px, "pz": pz - 1})
    first = jnp.where(even, px - 1, px + 1)
    last = jnp.where(even, px + 1, px - 1)
    x_first = ((first >= 0) & (first < nx), {"py": py, "px": first, "pz": pz})
    x_last = ((last >= 0) & (last < nx), {"py": py, "px": last, "pz": pz})
    neighbours = (y_up, y_down, z_up, z_down, x_first, x_last)

    def load(k):
        x0 = start_of(k)
        return (
            pltpu.make_async_copy(
                d_ref.at[:, pl.ds(x0, width)],
                field.at[0, pl.ds(1, Y), pl.ds(1 + x0, width), pl.ds(LOW, Z)],
                in_sem.at[k],
            ),
            pltpu.make_async_copy(c_ref.at[:, pl.ds(x0, width)], crowd.at[:, pl.ds(x0, width)], c_sem.at[k]),
        )

    for k in range(CHUNKS):
        load(k)[0].start()
    for k in range(CHUNKS):
        load(k)[1].start()

    zero_row = jnp.zeros((1, 128), jnp.float32)
    zero_plane = jnp.zeros((Z, 128), jnp.float32)

    def clear_rows(row):
        def one(i, _):
            y, x = 1 + i // X, 1 + lax.rem(i, X)
            for p in range(2):
                field[p, y, x, pl.ds(row, 1), :] = zero_row
            return 0

        lax.fori_loop(0, Y * X, one, 0)

    def clear_plane(y):
        def one(x, _):
            for p in range(2):
                field[p, y, 1 + x, pl.ds(LOW, Z), :] = zero_plane
            return 0

        lax.fori_loop(0, X, one, 0)

    def clear_column(x):
        def one(y, _):
            for p in range(2):
                field[p, 1 + y, x, pl.ds(LOW, Z), :] = zero_plane
            return 0

        lax.fori_loop(0, Y, one, 0)

    pl.when(pz == 0)(lambda: clear_rows(LOW - 1))
    pl.when(pz == nz - 1)(lambda: clear_rows(HIGH))
    pl.when(py == 0)(lambda: clear_plane(0))
    pl.when(py == ny - 1)(lambda: clear_plane(Y + 1))
    pl.when(px == 0)(lambda: clear_column(0))
    pl.when(px == nx - 1)(lambda: clear_column(X + 1))

    barrier = pltpu.get_barrier_semaphore()
    count = 0
    for exists, device in neighbours:
        count = count + exists.astype(jnp.int32)

        @pl.when(exists)
        def _():
            pl.semaphore_signal(barrier, inc=1, device_id=device, device_id_type=MESH)

    pl.semaphore_wait(barrier, count)

    def remote(src, dst, send, recv, device):
        return pltpu.make_async_remote_copy(src, dst, send, recv, device_id=device, device_id_type=MESH)

    def faces(p, k):
        xs = pl.ds(1 + start_of(k), width)
        ys, zs = pl.ds(1, Y), pl.ds(LOW, Z)
        f = field.at[p]
        return (
            (y_up[0], remote(f.at[Y, xs, zs], f.at[0, xs, zs], y_send.at[p, 0, k], y_recv.at[p, 0, k], y_up[1])),
            (y_down[0], remote(f.at[1, xs, zs], f.at[Y + 1, xs, zs], y_send.at[p, 1, k], y_recv.at[p, 1, k], y_down[1])),
            (z_up[0], remote(f.at[ys, xs, pl.ds(HIGH - 1, 1)], f.at[ys, xs, pl.ds(LOW - 1, 1)], z_send.at[p, 0, k], z_recv.at[p, 0, k], z_up[1])),
            (z_down[0], remote(f.at[ys, xs, pl.ds(LOW, 1)], f.at[ys, xs, pl.ds(HIGH, 1)], z_send.at[p, 1, k], z_recv.at[p, 1, k], z_down[1])),
        )

    def ends(p, side):
        ys, zs = pl.ds(1, Y), pl.ds(LOW, Z)
        f = field.at[p]
        low = even if side == 0 else jnp.logical_not(even)
        src, dst = jnp.where(low, 1, X), jnp.where(low, X + 1, 0)
        exists, device = x_first if side == 0 else x_last
        return exists, remote(f.at[ys, pl.ds(src, 1), zs], f.at[ys, pl.ds(dst, 1), zs], x_send.at[p, side], x_recv.at[p, side], device)

    def each(p, k, do_faces, do_ends):
        arrivals = (1, 0, 3, 2)
        fs = faces(p, k)
        for i, (exists, copy) in enumerate(fs):
            do_faces(exists, copy, fs[arrivals[i]][0])
        for side, at in ((0, 0), (1, CHUNKS - 1)):
            exists, copy = ends(p, side)
            pl.when(exists & (k == at))(lambda copy=copy: do_ends(copy))

    def send(p, k):
        each(p, k, lambda e, c, _: pl.when(e)(lambda: c.start()), lambda c: c.start())

    def sent(p, k):
        each(p, k, lambda e, c, _: pl.when(e)(lambda: c.wait_send()), lambda c: c.wait_send())

    def arrived(p, k):
        each(p, k, lambda _, c, e: pl.when(e)(lambda: c.wait_recv()), lambda c: c.wait_recv())

    def cells(p, y, x, z):
        return field[p, y, x, pl.ds(z, 8), :]

    def chunk(t, k, store):
        p = t % 2
        x0 = start_of(k)

        def column(i, _):
            x = x0 + i
            for z in range(LOW, HIGH, 8):
                line = [cells(p, y, 1 + x, z) for y in range(Y + 2)]
                out = []
                for y in range(1, Y + 1):
                    middle = line[y]
                    crowding = crowd[y - 1, x, pl.ds(z - LOW, 8), :]
                    near = (line[y - 1] + line[y + 1]) + (cells(p, y, x, z) + cells(p, y, x + 2, z))
                    near = near + (cells(p, y, 1 + x, z - 1) + cells(p, y, 1 + x, z + 1))
                    out.append(0.1 * (middle * (6.0 - 2.0 * crowding * middle) + near))
                store(x, z, out)
            return 0

        lax.fori_loop(0, width, column, 0)

    def first_send(k, _):
        load(k)[0].wait()
        send(0, k)
        return 0

    lax.fori_loop(0, CHUNKS, first_send, 0)

    for t in range(STEPS - 1):
        q = (t + 1) % 2

        def store(x, z, out):
            for y in range(Y):
                field[q, 1 + y, 1 + x, pl.ds(z, 8), :] = out[y]

        def step(k, _):
            arrived(t % 2, k)
            if t == 0:
                load(k)[1].wait()
            else:
                sent(q, k)
            chunk(t, k, store)
            send(q, k)
            return 0

        lax.fori_loop(0, CHUNKS, step, 0)

    def finish(x, z, out):
        here = None
        for y in range(Y):
            end_ref[y, x, pl.ds(z - LOW, 8), :] = out[y]
            here = out[y] if here is None else here + out[y]
            col_ref[y, x, pl.ds(z - LOW, 8), :] = here
        total[x, pl.ds(z - LOW, 8), :] = here

    def pass_on(k):
        xs = pl.ds(start_of(k), width)
        return remote(total.at[xs], below.at[xs], t_send.at[k], t_recv.at[k], y_up[1])

    def prefix(k):
        x0 = start_of(k)

        @pl.when(py > 0)
        def _():
            pass_on(k).wait_recv()

            def add(i, _):
                total[x0 + i] = total[x0 + i] + below[x0 + i]
                return 0

            lax.fori_loop(0, width, add, 0)

        @pl.when(py < ny - 1)
        def _():
            pass_on(k).start()

        scale = 1.0 / (Y * ny)

        def complete(i, _):
            lower = jnp.where(py > 0, below[x0 + i], 0.0)
            for y in range(Y):
                col_ref[y, x0 + i] = (col_ref[y, x0 + i] + lower) * scale
            return 0

        lax.fori_loop(0, width, complete, 0)

    half = py < ny // 2

    def last_step(k, _):
        arrived((STEPS - 1) % 2, k)
        chunk(STEPS - 1, k, finish)
        pl.when(half & (k > 0))(lambda: prefix(k - 1))
        return 0

    lax.fori_loop(0, CHUNKS, last_step, 0)
    pl.when(half)(lambda: prefix(CHUNKS - 1))

    @pl.when(jnp.logical_not(half))
    def _():
        def one(k, _):
            prefix(k)
            return 0

        lax.fori_loop(0, CHUNKS, one, 0)

    def drain(k, _):
        sent(0, k)
        sent(1, k)
        pl.when(py < ny - 1)(lambda: pass_on(k).wait_send())
        return 0

    lax.fori_loop(0, CHUNKS, drain, 0)


def solution(mesh):
    sizes = (mesh.shape["py"], mesh.shape["px"], mesh.shape["pz"])

    def local(density, crowding):
        Y, X, Z, S = density.shape
        dma = pltpu.SemaphoreType.DMA
        any_space = pl.BlockSpec(memory_space=pl.ANY)
        vmem = pl.BlockSpec(memory_space=pltpu.VMEM)
        return pl.pallas_call(
            functools.partial(kernel, sizes),
            out_shape=[jax.ShapeDtypeStruct(density.shape, jnp.float32)] * 2,
            in_specs=[any_space, any_space],
            out_specs=[vmem, vmem],
            scratch_shapes=[
                pltpu.VMEM((2, Y + 2, X + 2, Z + 16, S), jnp.float32),
                pltpu.VMEM((Y, X, Z, S), jnp.float32),
                pltpu.VMEM((X, Z, S), jnp.float32),
                pltpu.VMEM((X, Z, S), jnp.float32),
                dma((CHUNKS,)),
                dma((CHUNKS,)),
                dma((2, 2, CHUNKS)),
                dma((2, 2, CHUNKS)),
                dma((2, 2, CHUNKS)),
                dma((2, 2, CHUNKS)),
                dma((2, 2)),
                dma((2, 2)),
                dma((CHUNKS,)),
                dma((CHUNKS,)),
            ],
            compiler_params=pltpu.CompilerParams(
                collective_id=0, has_side_effects=True, vmem_limit_bytes=67_000_000
            ),
        )(density, crowding)

    spec = P("py", "px", "pz", None)
    return jax.shard_map(local, mesh=mesh, in_specs=(spec, spec), out_specs=(spec, spec), check_vma=False)
```

time: 402 us -> 126 us (0.31)
  other arithmetic: 163 us -> 0 us
  Pallas kernels: 0 us -> 114 us
  starting transfers between devices: 111 us -> 0 us
  waiting for transfers between devices: 68.1 us -> 0 us
  local copies, waits for them, and re-layouts: 41.6 us -> 11.4 us
  between operations: 14.7 us -> 0.65 us
    add x9 -> x0, other arithmetic: 147 us -> none  [the longest x6 142 us: march_step(): return middle + 0.1 * spread + 0.2 * middle * (1.0 - middle * crowding)]
    pallas_call x0 -> x1, Pallas kernels: none -> 114 us  [local(): pl.pallas_call(functools.partial(kernel, sizes), out_shape=[jax.ShapeDtyp...]
    ppermute x36 -> x0, starting transfers between devices: 111 us -> none  [the longest x18 56.2 us: with_halo(): lax.ppermute(last, axis, up)]
    all_gather x1 -> x0, waiting for transfers between devices: 44.5 us -> none  [entering(): gathered = lax.all_gather(part, axis)]
    slice x19 -> x0, local copies, waits for them, and re-layouts: 34.6 us -> none  [the longest x17 30.4 us: with_halo(): last = lax.slice_in_dim(array, length - width, length, axis=dim)]
    ppermute x36 -> x0, waiting for transfers between devices: 23.6 us -> none  [the longest x18 23.6 us: with_halo(): lax.ppermute(leading, axis, [(b, a) for a, b in up])]
    div x1 -> x0, other arithmetic: 8.49 us -> none  [local(): column_sum = (here + below) / (density.shape[0] * lax.axis_size('py'))]
    another operation x1 -> x0, other arithmetic: 7.88 us -> none  [local(): here = jnp.cumsum(density, axis=0)]
  transfers between devices with their start and end apart: 37 -> 0, of which waited for: 7 -> 0; matrix products, arithmetic and copies ran while one was open for 7% -> 0% of each run, Pallas kernels for 0% -> 0%
where the time goes in v1:
time: 126 us
  Pallas kernels  114 us (90%)
  local copies, waits for them, and re-layouts  11.4 us (9%)
    pallas_call x1, Pallas kernels, local(): pl.pallas_call(functools.partial(kernel, sizes), out_shape=[jax.ShapeDtyp...  114 us
    unnamed x4, local copies, waits for them, and re-layouts  11.4 us

profile of v1, /device:TPU:65, one launch (start us, length us, event | category | flops | bytes accessed | tf_op | source)
XLA Modules:
  0.0 126.0 jit_solution(11813044855970952591)
XLA Ops:
  0.6 114.0 %shard_map.41 = (f32[8,64,32,128]{3,2,1,0:T(8,128)}, f32[8,64,32,128]{3,2,1,0:T(8,128)}) custom-call(f32[8,64,32,128]{3,2,1,0:T(8,128)} %d_ref.1, f32[8,64,32,128]{3,2,1,0:T(8,128)} %c_ref.1), custom_call_target="tpu_custom_call" | custom-call | tf_op jit(solution)/shard_map/pallas_call | solution.py:263
  114.6 0.0 copy-start
  114.6 8.0 %copy.6 = f32[8,64,32,128]{3,2,1,0:T(8,128)} copy(f32[8,64,32,128]{3,2,1,0:T(8,128)} %get-tuple-element.4) | data formatting | bytes 16777216
  122.6 0.0 copy-done
  122.6 3.4 %copy.7 = f32[8,64,32,128]{3,2,1,0:T(8,128)} copy(f32[8,64,32,128]{3,2,1,0:T(8,128)S(1)} %copy-done) | data formatting | bytes 16777216
Async XLA Ops:
  114.6 8.0 %copy-start = (f32[8,64,32,128]{3,2,1,0:T(8,128)S(1)}, f32[8,64,32,128]{3,2,1,0:T(8,128)}, u32[]{:S(2)}) copy-start(f32[8,64,32,128]{3,2,1,0:T(8,128)} %get-tuple-element.5) | copy-start | bytes 25165828

commit v2 on v1

--- a/solution.py
+++ b/solution.py
@@ -9,29 +9,37 @@
 
 STEPS = 6
 CHUNKS = 8
+FORWARD_AT = 2
 MESH = pl.DeviceIdType.MESH
 LOW, HIGH = 8, 40
 
 
 def kernel(sizes, d_ref, c_ref, col_ref, end_ref, field, crowd, below, total,
-           in_sem, c_sem, y_send, y_recv, z_send, z_recv, x_send, x_recv, t_send, t_recv):
+           hop, in_sem, c_sem, y_send, y_recv, z_send, z_recv, x_send, x_recv, t_send, t_recv,
+           far_send, far_recv, hop_recv, relay_send):
     ny, nx, nz = sizes
     py, px, pz = lax.axis_index("py"), lax.axis_index("px"), lax.axis_index("pz")
     Y, X, Z, _ = d_ref.shape
     width = X // CHUNKS
-    even = lax.rem(px, 2) == 0
+    upward = lax.rem(px, 2) == 1
+    half_x = nx // 2
+    part = Y // half_x
+    near = (px == half_x - 1) | (px == half_x)
+    lane = jnp.where(px < half_x, half_x - 1 - px, px - half_x)
+    beside = {"py": py, "px": jnp.where(px < half_x, half_x - 1, half_x), "pz": pz}
+    across = {"py": py, "px": jnp.where(px < half_x, half_x, half_x - 1), "pz": pz}
 
     def start_of(k):
-        return pl.multiple_of(jnp.where(even, k, CHUNKS - 1 - k) * width, width)
+        return pl.multiple_of(jnp.where(upward, k, CHUNKS - 1 - k) * width, width)
 
     y_up = (py < ny - 1, {"py": py + 1, "px": px, "pz": pz})
     y_down = (py > 0, {"py": py - 1, "px": px, "pz": pz})
     z_up = (pz < nz - 1, {"py": py, "px": px, "pz": pz + 1})
     z_down = (pz > 0, {"py": py, "px": px, "pz": pz - 1})
-    first = jnp.where(even, px - 1, px + 1)
-    last = jnp.where(even, px + 1, px - 1)
+    first = jnp.where(upward, px - 1, px + 1)
+    last = jnp.where(upward, px + 1, px - 1)
     x_first = ((first >= 0) & (first < nx), {"py": py, "px": first, "pz": pz})
-    x_last = ((last >= 0) & (last < nx), {"py": py, "px": last, "pz": pz})
+    x_last = ((last >= 0) & (last < nx) & jnp.logical_not(near), {"py": py, "px": last, "pz": pz})
     neighbours = (y_up, y_down, z_up, z_down, x_first, x_last)
 
     def load(k):
@@ -50,41 +58,6 @@
     for k in range(CHUNKS):
         load(k)[1].start()
 
-    zero_row = jnp.zeros((1, 128), jnp.float32)
-    zero_plane = jnp.zeros((Z, 128), jnp.float32)
-
-    def clear_rows(row):
-        def one(i, _):
-            y, x = 1 + i // X, 1 + lax.rem(i, X)
-            for p in range(2):
-                field[p, y, x, pl.ds(row, 1), :] = zero_row
-            return 0
-
-        lax.fori_loop(0, Y * X, one, 0)
-
-    def clear_plane(y):
-        def one(x, _):
-            for p in range(2):
-                field[p, y, 1 + x, pl.ds(LOW, Z), :] = zero_plane
-            return 0
-
-        lax.fori_loop(0, X, one, 0)
-
-    def clear_column(x):
-        def one(y, _):
-            for p in range(2):
-                field[p, 1 + y, x, pl.ds(LOW, Z), :] = zero_plane
-            return 0
-
-        lax.fori_loop(0, Y, one, 0)
-
-    pl.when(pz == 0)(lambda: clear_rows(LOW - 1))
-    pl.when(pz == nz - 1)(lambda: clear_rows(HIGH))
-    pl.when(py == 0)(lambda: clear_plane(0))
-    pl.when(py == ny - 1)(lambda: clear_plane(Y + 1))
-    pl.when(px == 0)(lambda: clear_column(0))
-    pl.when(px == nx - 1)(lambda: clear_column(X + 1))
-
     barrier = pltpu.get_barrier_semaphore()
     count = 0
     for exists, device in neighbours:
@@ -92,6 +65,20 @@
 
         @pl.when(exists)
         def _():
+            pl.semaphore_signal(barrier, inc=1, device_id=device, device_id_type=MESH)
+
+    ends_of_face = tuple({"py": py, "px": half_x - 1 + i, "pz": pz} for i in range(2))
+    relays = tuple({"py": py, "px": x, "pz": pz} for x in range(nx) if x not in (half_x - 1, half_x))
+    count = count + jnp.where(near, len(relays) + 1, len(ends_of_face))
+
+    @pl.when(near)
+    def _():
+        for device in (*relays, across):
+            pl.semaphore_signal(barrier, inc=1, device_id=device, device_id_type=MESH)
+
+    @pl.when(jnp.logical_not(near))
+    def _():
+        for device in ends_of_face:
             pl.semaphore_signal(barrier, inc=1, device_id=device, device_id_type=MESH)
 
     pl.semaphore_wait(barrier, count)
@@ -113,10 +100,39 @@
     def ends(p, side):
         ys, zs = pl.ds(1, Y), pl.ds(LOW, Z)
         f = field.at[p]
-        low = even if side == 0 else jnp.logical_not(even)
+        low = upward if side == 0 else jnp.logical_not(upward)
         src, dst = jnp.where(low, 1, X), jnp.where(low, X + 1, 0)
         exists, device = x_first if side == 0 else x_last
         return exists, remote(f.at[ys, pl.ds(src, 1), zs], f.at[ys, pl.ds(dst, 1), zs], x_send.at[p, side], x_recv.at[p, side], device)
+
+    def part_of(p, x, which):
+        return field.at[p, pl.ds(1 + which * part, part), pl.ds(x, 1), pl.ds(LOW, Z)]
+
+    def far(t, which):
+        p = t % 2
+        low = px == half_x
+        src, dst = jnp.where(low, 1, X), jnp.where(low, X + 1, 0)
+        if which == 0:
+            return remote(part_of(p, src, 0), part_of(p, dst, 0), far_send.at[p, 0], far_recv.at[p, 0], across)
+        relay = {"py": py, "px": jnp.where(low, half_x - 1 - which, half_x + which), "pz": pz}
+        return remote(part_of(p, src, which), hop.at[t], far_send.at[p, which], hop_recv.at[t], relay)
+
+    def far_in(t, which):
+        p = t % 2
+        x = jnp.where(px == half_x, 0, X + 1)
+        return remote(part_of(p, x, which), part_of(p, x, which), far_send.at[p, which], far_recv.at[p, which], across)
+
+    def onward(t):
+        p = t % 2
+        dst = part_of(p, jnp.where(px < half_x, X + 1, 0), lane)
+        return remote(hop.at[t], dst, relay_send.at[t], far_recv.at[p, lane], beside)
+
+    def forward(t, k):
+        @pl.when(jnp.logical_not(near) & (k == FORWARD_AT))
+        def _():
+            copy = onward(t)
+            remote(hop.at[t], hop.at[t], relay_send.at[t], hop_recv.at[t], across).wait_recv()
+            copy.start()
 
     def each(p, k, do_faces, do_ends):
         arrivals = (1, 0, 3, 2)
@@ -127,14 +143,29 @@
             exists, copy = ends(p, side)
             pl.when(exists & (k == at))(lambda copy=copy: do_ends(copy))
 
-    def send(p, k):
-        each(p, k, lambda e, c, _: pl.when(e)(lambda: c.start()), lambda c: c.start())
-
-    def sent(p, k):
-        each(p, k, lambda e, c, _: pl.when(e)(lambda: c.wait_send()), lambda c: c.wait_send())
-
-    def arrived(p, k):
-        each(p, k, lambda _, c, e: pl.when(e)(lambda: c.wait_recv()), lambda c: c.wait_recv())
+    def send(t, k):
+        each(t % 2, k, lambda e, c, _: pl.when(e)(lambda: c.start()), lambda c: c.start())
+
+        @pl.when(near & (k == CHUNKS - 1))
+        def _():
+            for which in range(half_x):
+                far(t, which).start()
+
+    def sent(t, k):
+        each(t % 2, k, lambda e, c, _: pl.when(e)(lambda: c.wait_send()), lambda c: c.wait_send())
+
+        @pl.when(near & (k == CHUNKS - 1))
+        def _():
+            for which in range(half_x):
+                far(t, which).wait_send()
+
+    def arrived(t, k):
+        each(t % 2, k, lambda _, c, e: pl.when(e)(lambda: c.wait_recv()), lambda c: c.wait_recv())
+
+        @pl.when(near & (k == CHUNKS - 1))
+        def _():
+            for which in range(half_x):
+                far_in(t, which).wait_recv()
 
     def cells(p, y, x, z):
         return field[p, y, x, pl.ds(z, 8), :]
@@ -166,6 +197,38 @@
 
     lax.fori_loop(0, CHUNKS, first_send, 0)
 
+    zero_row = jnp.zeros((1, 128), jnp.float32)
+    zero_plane = jnp.zeros((Z, 128), jnp.float32)
+
+    def clear_rows(row):
+        def one(x, _):
+            for p in range(2):
+                for y in range(1, Y + 1):
+                    field[p, y, 1 + x, pl.ds(row, 1), :] = zero_row
+            return 0
+
+        lax.fori_loop(0, X, one, 0)
+
+    def clear_plane(y):
+        def one(x, _):
+            for p in range(2):
+                field[p, y, 1 + x, pl.ds(LOW, Z), :] = zero_plane
+            return 0
+
+        lax.fori_loop(0, X, one, 0)
+
+    def clear_column(x):
+        for p in range(2):
+            for y in range(1, Y + 1):
+                field[p, y, x, pl.ds(LOW, Z), :] = zero_plane
+
+    pl.when(pz == 0)(lambda: clear_rows(LOW - 1))
+    pl.when(pz == nz - 1)(lambda: clear_rows(HIGH))
+    pl.when(py == 0)(lambda: clear_plane(0))
+    pl.when(py == ny - 1)(lambda: clear_plane(Y + 1))
+    pl.when(px == 0)(lambda: clear_column(0))
+    pl.when(px == nx - 1)(lambda: clear_column(X + 1))
+
     for t in range(STEPS - 1):
         q = (t + 1) % 2
 
@@ -174,13 +237,14 @@
                 field[q, 1 + y, 1 + x, pl.ds(z, 8), :] = out[y]
 
         def step(k, _):
-            arrived(t % 2, k)
+            arrived(t, k)
             if t == 0:
                 load(k)[1].wait()
             else:
-                sent(q, k)
+                sent(t - 1, k)
             chunk(t, k, store)
-            send(q, k)
+            send(t + 1, k)
+            forward(t, k)
             return 0
 
         lax.fori_loop(0, CHUNKS, step, 0)
@@ -227,8 +291,9 @@
     half = py < ny // 2
 
     def last_step(k, _):
-        arrived((STEPS - 1) % 2, k)
+        arrived(STEPS - 1, k)
         chunk(STEPS - 1, k, finish)
+        forward(STEPS - 1, k)
         pl.when(half & (k > 0))(lambda: prefix(k - 1))
         return 0
 
@@ -244,12 +309,27 @@
         lax.fori_loop(0, CHUNKS, one, 0)
 
     def drain(k, _):
-        sent(0, k)
-        sent(1, k)
+        sent(STEPS - 2, k)
+        sent(STEPS - 1, k)
         pl.when(py < ny - 1)(lambda: pass_on(k).wait_send())
         return 0
 
     lax.fori_loop(0, CHUNKS, drain, 0)
+
+    @pl.when(jnp.logical_not(near))
+    def _():
+        for t in range(STEPS):
+            onward(t).wait_send()
+
+
+def write_out(col_ref, end_ref, col_out, end_out, sem):
+    copies = [
+        pltpu.make_async_copy(end_ref.at[y], end_out.at[y], sem.at[0, y]) for y in range(end_ref.shape[0])
+    ] + [pltpu.make_async_copy(col_ref.at[y], col_out.at[y], sem.at[1, y]) for y in range(col_ref.shape[0])]
+    for copy in copies:
+        copy.start()
+    for copy in copies:
+        copy.wait()
 
 
 def solution(mesh):
@@ -260,9 +340,9 @@
         dma = pltpu.SemaphoreType.DMA
         any_space = pl.BlockSpec(memory_space=pl.ANY)
         vmem = pl.BlockSpec(memory_space=pltpu.VMEM)
-        return pl.pallas_call(
+        column_sum, end = pl.pallas_call(
             functools.partial(kernel, sizes),
-            out_shape=[jax.ShapeDtypeStruct(density.shape, jnp.float32)] * 2,
+            out_shape=[pltpu.VMEM(density.shape, jnp.float32)] * 2,
             in_specs=[any_space, any_space],
             out_specs=[vmem, vmem],
             scratch_shapes=[
@@ -270,6 +350,7 @@
                 pltpu.VMEM((Y, X, Z, S), jnp.float32),
                 pltpu.VMEM((X, Z, S), jnp.float32),
                 pltpu.VMEM((X, Z, S), jnp.float32),
+                pltpu.VMEM((STEPS, Y // (sizes[1] // 2), 1, Z, S), jnp.float32),
                 dma((CHUNKS,)),
                 dma((CHUNKS,)),
                 dma((2, 2, CHUNKS)),
@@ -280,11 +361,23 @@
                 dma((2, 2)),
                 dma((CHUNKS,)),
                 dma((CHUNKS,)),
+                dma((2, sizes[1] // 2)),
+                dma((2, sizes[1] // 2)),
+                dma((STEPS,)),
+                dma((STEPS,)),
             ],
             compiler_params=pltpu.CompilerParams(
-                collective_id=0, has_side_effects=True, vmem_limit_bytes=67_000_000
+                collective_id=0, has_side_effects=True, vmem_limit_bytes=45_500_000
             ),
         )(density, crowding)
+        return pl.pallas_call(
+            write_out,
+            out_shape=[jax.ShapeDtypeStruct(density.shape, jnp.float32)] * 2,
+            in_specs=[vmem, vmem],
+            out_specs=[any_space, any_space],
+            scratch_shapes=[dma((2, Y))],
+            compiler_params=pltpu.CompilerParams(vmem_limit_bytes=4_000_000),
+        )(column_sum, end)
 
     spec = P("py", "px", "pz", None)
     return jax.shard_map(local, mesh=mesh, in_specs=(spec, spec), out_specs=(spec, spec), check_vma=False)

time: 126 us -> 98.4 us (0.78)
  Pallas kernels: 114 us -> 97.6 us
  local copies, waits for them, and re-layouts: 11.4 us -> 0 us
    pallas_call x1 -> x2, Pallas kernels: 114 us -> 97.6 us  [the longest x1 91.7 us: local(): pl.pallas_call(functools.partial(kernel, sizes), out_shape=[pltpu.VMEM(de...]
    unnamed x4 -> x0, local copies, waits for them, and re-layouts: 11.4 us -> none
where the time goes in v2:
time: 98.4 us; the launch traced here: 98.3 us
  Pallas kernels  97.6 us (99%)
    pallas_call x1, Pallas kernels, local(): pl.pallas_call(functools.partial(kernel, sizes), out_shape=[pltpu.VMEM(de...  91.7 us
    pallas_call x1, Pallas kernels, local(): pl.pallas_call(write_out, out_shape=[jax.ShapeDtypeStruct(density.shape,...  5.96 us

profile of v2, /device:TPU:65, one launch (start us, length us, event | category | flops | bytes accessed | tf_op | source)
XLA Modules:
  0.0 98.3 jit_solution(15392319389998733271)
XLA Ops:
  0.6 91.7 %shard_map.41 = (f32[8,64,32,128]{3,2,1,0:T(8,128)S(1)}, f32[8,64,32,128]{3,2,1,0:T(8,128)S(1)}) custom-call(f32[8,64,32,128]{3,2,1,0:T(8,128)} %d_ref.1, f32[8,64,32,128]{3,2,1,0:T(8,128)} %c_ref.1), custom_call_target="tpu_custom_call" | custom-call | tf_op jit(solution)/shard_map/pallas_call | solution.py:343
  92.3 6.0 %shard_map.42 = (f32[8,64,32,128]{3,2,1,0:T(8,128)}, f32[8,64,32,128]{3,2,1,0:T(8,128)}) custom-call(f32[8,64,32,128]{3,2,1,0:T(8,128)S(1)} %get-tuple-element.4.col_ref, f32[8,64,32,128]{3,2,1,0:T(8,128)S(1)} %get-tuple-element.5.end_ref), custom_call_target="tpu_custom_call" | custom-call | tf_op jit(solution)/shard_map/pallas_call | solution.py:373

commit v3 on v2

--- a/solution.py
+++ b/solution.py
@@ -53,11 +53,6 @@
             pltpu.make_async_copy(c_ref.at[:, pl.ds(x0, width)], crowd.at[:, pl.ds(x0, width)], c_sem.at[k]),
         )
 
-    for k in range(CHUNKS):
-        load(k)[0].start()
-    for k in range(CHUNKS):
-        load(k)[1].start()
-
     barrier = pltpu.get_barrier_semaphore()
     count = 0
     for exists, device in neighbours:
@@ -81,6 +76,8 @@
         for device in ends_of_face:
             pl.semaphore_signal(barrier, inc=1, device_id=device, device_id_type=MESH)
 
+    for k in range(CHUNKS):
+        load(k)[0].start()
     pl.semaphore_wait(barrier, count)
 
     def remote(src, dst, send, recv, device):
@@ -196,6 +193,8 @@
         return 0
 
     lax.fori_loop(0, CHUNKS, first_send, 0)
+    for k in range(CHUNKS):
+        load(k)[1].start()
 
     zero_row = jnp.zeros((1, 128), jnp.float32)
     zero_plane = jnp.zeros((Z, 128), jnp.float32)
@@ -300,18 +299,9 @@
     lax.fori_loop(0, CHUNKS, last_step, 0)
     pl.when(half)(lambda: prefix(CHUNKS - 1))
 
-    @pl.when(jnp.logical_not(half))
-    def _():
-        def one(k, _):
-            prefix(k)
-            return 0
-
-        lax.fori_loop(0, CHUNKS, one, 0)
-
     def drain(k, _):
         sent(STEPS - 2, k)
         sent(STEPS - 1, k)
-        pl.when(py < ny - 1)(lambda: pass_on(k).wait_send())
         return 0
 
     lax.fori_loop(0, CHUNKS, drain, 0)
@@ -320,6 +310,22 @@
     def _():
         for t in range(STEPS):
             onward(t).wait_send()
+
+    @pl.when(jnp.logical_not(half))
+    def _():
+        def one(k, _):
+            prefix(k)
+            return 0
+
+        lax.fori_loop(0, CHUNKS, one, 0)
+
+    @pl.when(py < ny - 1)
+    def _():
+        def out(k, _):
+            pass_on(k).wait_send()
+            return 0
+
+        lax.fori_loop(0, CHUNKS, out, 0)
 
 
 def write_out(col_ref, end_ref, col_out, end_out, sem):

time: 98.4 us -> 98 us (level)
  no operation moved by 1% of the time
where the time goes in v3:
time: 98 us; the launch traced here: 97.9 us
  Pallas kernels  97.2 us (99%)
    pallas_call x1, Pallas kernels, local(): pl.pallas_call(functools.partial(kernel, sizes), out_shape=[pltpu.VMEM(de...  91.3 us
    pallas_call x1, Pallas kernels, local(): pl.pallas_call(write_out, out_shape=[jax.ShapeDtypeStruct(density.shape,...  5.96 us

profile of v3, /device:TPU:65, one launch (start us, length us, event | category | flops | bytes accessed | tf_op | source)
XLA Modules:
  0.0 97.9 jit_solution(17288652601293150390)
XLA Ops:
  0.6 91.3 %shard_map.41 = (f32[8,64,32,128]{3,2,1,0:T(8,128)S(1)}, f32[8,64,32,128]{3,2,1,0:T(8,128)S(1)}) custom-call(f32[8,64,32,128]{3,2,1,0:T(8,128)} %d_ref.1, f32[8,64,32,128]{3,2,1,0:T(8,128)} %c_ref.1), custom_call_target="tpu_custom_call" | custom-call | tf_op jit(solution)/shard_map/pallas_call | solution.py:349
  91.9 6.0 %shard_map.42 = (f32[8,64,32,128]{3,2,1,0:T(8,128)}, f32[8,64,32,128]{3,2,1,0:T(8,128)}) custom-call(f32[8,64,32,128]{3,2,1,0:T(8,128)S(1)} %get-tuple-element.4.col_ref, f32[8,64,32,128]{3,2,1,0:T(8,128)S(1)} %get-tuple-element.5.end_ref), custom_call_target="tpu_custom_call" | custom-call | tf_op jit(solution)/shard_map/pallas_call | solution.py:379

commit v4 on v3

--- a/solution.py
+++ b/solution.py
@@ -9,7 +9,7 @@
 
 STEPS = 6
 CHUNKS = 8
-FORWARD_AT = 2
+FORWARD_AT = 3
 MESH = pl.DeviceIdType.MESH
 LOW, HIGH = 8, 40
 
@@ -271,7 +271,9 @@
                 total[x0 + i] = total[x0 + i] + below[x0 + i]
                 return 0
 
-            lax.fori_loop(0, width, add, 0)
+            @pl.when(py < ny - 1)
+            def _():
+                lax.fori_loop(0, width, add, 0)
 
         @pl.when(py < ny - 1)
         def _():

time: 98 us -> 97.6 us (level)
  no operation moved by 1% of the time
where the time goes in v4:
time: 97.6 us; the launch traced here: 97.5 us
  Pallas kernels  96.9 us (99%)
    pallas_call x1, Pallas kernels, local(): pl.pallas_call(functools.partial(kernel, sizes), out_shape=[pltpu.VMEM(de...  90.9 us
    pallas_call x1, Pallas kernels, local(): pl.pallas_call(write_out, out_shape=[jax.ShapeDtypeStruct(density.shape,...  5.96 us

profile of v4, /device:TPU:65, one launch (start us, length us, event | category | flops | bytes accessed | tf_op | source)
XLA Modules:
  0.0 97.5 jit_solution(5729593776015754340)
XLA Ops:
  0.6 90.9 %shard_map.41 = (f32[8,64,32,128]{3,2,1,0:T(8,128)S(1)}, f32[8,64,32,128]{3,2,1,0:T(8,128)S(1)}) custom-call(f32[8,64,32,128]{3,2,1,0:T(8,128)} %d_ref.1, f32[8,64,32,128]{3,2,1,0:T(8,128)} %c_ref.1), custom_call_target="tpu_custom_call" | custom-call | tf_op jit(solution)/shard_map/pallas_call | solution.py:351
  91.5 6.0 %shard_map.42 = (f32[8,64,32,128]{3,2,1,0:T(8,128)}, f32[8,64,32,128]{3,2,1,0:T(8,128)}) custom-call(f32[8,64,32,128]{3,2,1,0:T(8,128)S(1)} %get-tuple-element.4.col_ref, f32[8,64,32,128]{3,2,1,0:T(8,128)S(1)} %get-tuple-element.5.end_ref), custom_call_target="tpu_custom_call" | custom-call | tf_op jit(solution)/shard_map/pallas_call | solution.py:381
